TPU v7x, 32 devices: a whole 2x2x4 slice. The times are simulated.
32 devices in a mesh: dom: 8 (over y, x, core), rep: 4 (over z).
Axes of the slice: x: 2, y: 2, z: 4, core: 2. Of those that a mesh axis runs over, the one named last changes fastest.
Arguments:
- right_sides: float32 [4, 48, 16, 384], P(None, 'dom', 'rep'), may hold values from -6 to 6
- diag_inverse: bfloat16 [4, 48, 384, 384], P(None, 'dom'), may hold values from -0.3125 to 0.3125
- panel_mats: bfloat16 [3, 512, 384, 384], P(None, ('dom', 'rep')), may hold values from -0.08984375 to 0.08984375
- panel_src: int32 [3, 512], P(None, ('dom', 'rep')), may hold values from 0 to 17, as said below
- panel_dst: int32 [3, 512], P(None, ('dom', 'rep')), may hold values from -1 to 47, as said below
Outputs:
- solution: float32 [4, 48, 16, 384], P(None, 'dom', 'rep')
Inputs may be any that keep to these rules, and one draw needn't show every extreme that they name: `panel_src`: an entry of row l is below (l + 1) * 6, so the source tile lies in a level at most l; most of the entries lie in level l itself. A live entry of a list owned by dom index o names a tile of dom index (o + j) mod 8 with -2 <= j <= 2 or j = 4. Among the 16 entries of one device's list for one row, at most 3 live entries have the same destination dom index (panel_dst // 6), and in every list some dom index has exactly 3; lists of low dom indices tend to hold more live entries than those of high ones.
All inputs are finite; a program needn't handle non-finite values.
Results may differ from a plain program's by a relative error of at most 0.012.
Values may be sent and summed in bfloat16 or wider, within the bound.
A program may use at most 128 MiB of HBM per device.

v0:
```python
import functools

import jax
import jax.numpy as jnp
import numpy as np
from jax import lax
from jax.experimental import pallas as pl
from jax.experimental.pallas import tpu as pltpu
from jax.sharding import PartitionSpec as P

HALF = 2
SLOTS = 3
HOOD = 2 * HALF + 2
MESH = pl.DeviceIdType.MESH
F32 = jnp.float32
BF16 = jnp.bfloat16


def round_up(value, unit):
    return -(-value // unit) * unit


def iota(shape, dim):
    return lax.broadcasted_iota(jnp.int32, shape, dim).astype(F32)


def lane_tables(rep_size, panel_count, col_count):
    rhs = rep_size * col_count
    half = 2 * col_count
    width = max(panel_count * rhs, HOOD * rep_size * half, 128)
    lane = np.arange(width)
    return np.stack(
        [
            lane // rhs,
            (lane % rhs) // col_count * half + lane % col_count,
            lane // (2 * half),
            (lane % (2 * half)) // col_count,
            lane % col_count,
            lane // half,
            lane % half,
            (lane + col_count) % half,
        ]
    ).astype(np.float32)


def regroup_table(rep_size, tile_count, col_count, group_rows):
    table = np.zeros((tile_count * rep_size * col_count, rep_size * group_rows), np.float32)
    for r in range(rep_size):
        for t in range(tile_count):
            for c in range(col_count):
                table[(t * rep_size + r) * col_count + c, r * group_rows + t * col_count + c] = 1
    return table


def kernel(
    dims,
    src_hbm, dst_hbm, rs_hbm, lanes_hbm, regroup_hbm, diag_hbm, panel_hbm,
    out_ref,
    src_ref, dst_ref, rs_ref, lanes_ref, regroup_ref, small_sem,
    diag, panel, store, contrib, pack, unpack,
    solved_send, solved_recv, val_send, val_recv, id_send, id_recv,
    diag_sem, panel_sem, solved_ssem, solved_rsem, val_ssem, val_rsem, id_ssem, id_rsem,
):
    levels, tiles, cols, width, panels, dom_size, rep_size, group_rows, chunk = dims
    far = dom_size // 2
    rhs = rep_size * cols
    half = 2 * cols
    fold = width // 3 * 2
    tile_rows = tiles * cols
    me_d = lax.axis_index("dom")
    me_r = lax.axis_index("rep")
    offsets = [o - HALF for o in range(HOOD - 1)] + [far]
    senders = HOOD * rep_size

    def peer_dom(offset):
        return lax.rem(me_d + (offset + dom_size), dom_size)

    def peer_rep(step):
        return lax.rem(me_r + step, rep_size)

    far_first = sorted(range(1, rep_size), key=lambda s: (-min(s, rep_size - s), -s))
    peers = [
        (j, step)
        for j in (HOOD - 1, 0, HOOD - 2, 1, HOOD - 3, HALF)
        for step in range(rep_size - 1, -1, -1)
        if (offsets[j], step) != (0, 0)
    ]

    def load_diag(level):
        return pltpu.make_async_copy(diag_hbm.at[level], diag.at[level], diag_sem.at[level])

    def load_panel(level, part):
        span = pl.ds(part * chunk, chunk)
        return pltpu.make_async_copy(
            panel_hbm.at[level, span], panel.at[level, span], panel_sem.at[level, part]
        )

    def send_id(j, step):
        return pltpu.make_async_remote_copy(
            src_ref=id_send.at[j],
            dst_ref=id_recv.at[j * rep_size + me_r],
            send_sem=id_ssem.at[j * rep_size + step],
            recv_sem=id_rsem.at[j * rep_size + me_r],
            device_id=(peer_dom(offsets[j]), peer_rep(step)),
            device_id_type=MESH,
        )

    def await_id(j, step):
        slot = j * rep_size + peer_rep(step)
        pltpu.make_async_remote_copy(
            src_ref=id_send.at[j],
            dst_ref=id_recv.at[slot],
            send_sem=id_ssem.at[j * rep_size + step],
            recv_sem=id_rsem.at[slot],
            device_id=(peer_dom(-offsets[j]), peer_rep(step)),
            device_id_type=MESH,
        ).wait_recv()


    def rows_of(slot):
        return pl.ds(pl.multiple_of(slot * half, half), half)

    def send_val(level, j, step):
        return pltpu.make_async_remote_copy(
            src_ref=val_send.at[level, rows_of(j * rep_size + peer_rep(step))],
            dst_ref=val_recv.at[level, rows_of(j * rep_size + me_r)],
            send_sem=val_ssem.at[level, j * rep_size + step],
            recv_sem=val_rsem.at[level, j * rep_size + me_r],
            device_id=(peer_dom(offsets[j]), peer_rep(step)),
            device_id_type=MESH,
        )

    def await_val(level, j, step):
        slot = j * rep_size + peer_rep(step)
        pltpu.make_async_remote_copy(
            src_ref=val_send.at[level, rows_of(slot)],
            dst_ref=val_recv.at[level, rows_of(slot)],
            send_sem=val_ssem.at[level, j * rep_size + step],
            recv_sem=val_rsem.at[level, slot],
            device_id=(peer_dom(-offsets[j]), peer_rep(step)),
            device_id_type=MESH,
        ).wait_recv()

    tile_span = pl.ds(0, tile_rows)

    def send_solved(level, step):
        return pltpu.make_async_remote_copy(
            src_ref=solved_send.at[level, tile_span],
            dst_ref=solved_recv.at[level, me_r, tile_span],
            send_sem=solved_ssem.at[level, step],
            recv_sem=solved_rsem.at[level, me_r],
            device_id=(me_d, peer_rep(step)),
            device_id_type=MESH,
        )

    def await_solved(level, step):
        slot = peer_rep(step)
        pltpu.make_async_remote_copy(
            src_ref=solved_send.at[level, tile_span],
            dst_ref=solved_recv.at[level, slot, tile_span],
            send_sem=solved_ssem.at[level, step],
            recv_sem=solved_rsem.at[level, slot],
            device_id=(me_d, slot),
            device_id_type=MESH,
        ).wait_recv()

    small = [
        pltpu.make_async_copy(hbm, ref, small_sem.at[i])
        for i, (hbm, ref) in enumerate(
            (
                (dst_hbm, dst_ref),
                (lanes_hbm, lanes_ref),
                (rs_hbm, rs_ref),
                (regroup_hbm, regroup_ref),
                (src_hbm, src_ref),
            )
        )
    ]
    small[0].start()
    small[1].start()
    load_diag(0).start()
    for copy in small[2:]:
        copy.start()

    solved_recv[...] = jnp.zeros_like(solved_recv)

    barrier = pltpu.get_barrier_semaphore()
    for j, step in peers:
        pl.semaphore_signal(
            barrier,
            inc=1,
            device_id=(peer_dom(offsets[j]), peer_rep(step)),
            device_id_type=MESH,
        )

    def route():
        owner = me_d.astype(F32)
        lane_panel = lanes_ref[0:1, : panels * rhs]
        lane_row = lanes_ref[1:2, : panels * rhs]
        id_level = lanes_ref[2:3, :128]
        id_slot = lanes_ref[3:4, :128]
        id_col = lanes_ref[4:5, :128]
        row16 = iota((panels, panels), 0)
        col16 = iota((panels, panels), 1)
        wanted = [jnp.zeros((1, 128), F32) for _ in range(HOOD)]
        for l in range(levels - 1):
            drow = dst_ref[l : l + 1, :].astype(F32)
            dcol = jnp.sum(jnp.where(row16 == col16, drow, 0.0), axis=1, keepdims=True)
            trow = jnp.where(drow >= 0, jnp.floor((drow + 0.5) * (1.0 / tiles)), -1.0)
            tcol = jnp.where(dcol >= 0, jnp.floor((dcol + 0.5) * (1.0 / tiles)), -1.0)
            earlier = (tcol == trow) & (drow >= 0) & (col16 < row16)
            rank = jnp.sum(jnp.where(earlier, 1.0, 0.0), axis=1, keepdims=True)
            away = tcol - owner
            away = away + jnp.where(away < 0, float(dom_size), 0.0)
            near = away + HALF
            near = near - jnp.where(near >= dom_size, float(dom_size), 0.0)
            reach = jnp.where(away == far, float(HOOD - 1), near)
            reach = jnp.where(dcol >= 0, reach, -1.0)
            start = reach * (rep_size * half)
            first = jnp.where((dcol >= 0) & (rank < 2), start + rank * cols, -1.0e6)
            third = jnp.where((dcol >= 0) & (rank == 2), start + senders * half, -1.0e6)
            tile = dcol - tiles * tcol
            here = iota((panels, panels * rhs), 0) == lane_panel
            goal = jnp.sum(jnp.where(here, first, 0.0), axis=0, keepdims=True) + lane_row
            fold_goal = jnp.sum(jnp.where(here, third, 0.0), axis=0, keepdims=True) + lane_row
            row = iota((2 * senders * half, panels * rhs), 0)
            hit = (row == goal) | (row == fold_goal) | (row == fold_goal + cols)
            pack[l] = jnp.where(hit, 1.0, 0.0).astype(BF16)
            mine = (rank == id_slot) & (id_level == l)
            for j in range(HOOD):
                found = jnp.where(mine & (reach == j), tile + 1.0, 0.0)
                wanted[j] = wanted[j] + jnp.sum(found, axis=0, keepdims=True)
        for j in range(HOOD):
            row = jnp.where(wanted[j] > 0, (wanted[j] - 1.0) * cols + id_col, -1.0)
            id_send[j] = row.astype(jnp.int32)
        id_recv[HALF * rep_size + me_r] = id_send[HALF]

    def learn_ids():
        for j, step in peers:
            await_id(j, step)
        row_of = iota((senders, 128), 0)
        ids = jnp.zeros((senders, 128), F32)
        for s in range(senders):
            ids = jnp.where(row_of == s, id_recv[s].astype(F32), ids)
        ids = ids.astype(BF16)
        span = senders * half
        lane_sender = lanes_ref[5:6, :span]
        lane_in = lanes_ref[6:7, :span]
        lane_turned = lanes_ref[7:8, :span]
        for l in range(levels - 1):
            start = l * 2 * half
            for k, lane in enumerate((lane_in + start, lane_in + (start + half), lane_turned + (start + half))):
                take = jnp.where(iota((128, span), 0) == lane, 1.0, 0.0)
                every = jnp.dot(ids, take.astype(BF16), preferred_element_type=F32)
                own = jnp.where(iota((senders, span), 0) == lane_sender, every, 0.0)
                goal = jnp.sum(own, axis=0, keepdims=True)
                unpack[l, k] = jnp.where(iota((tile_rows, span), 0) == goal, 1.0, 0.0).astype(BF16)

    def solve(level, residual):
        row_tile = lax.broadcasted_iota(jnp.int32, (tile_rows, width), 0)
        total = jnp.zeros((tile_rows, width), F32)
        for t in range(tiles):
            inside = (row_tile >= t * cols) & (row_tile < (t + 1) * cols)
            part = jnp.where(inside, residual, 0.0).astype(BF16)
            total = total + jnp.dot(part, diag[level, t], preferred_element_type=F32)
        return total

    small[0].wait()
    small[1].wait()
    route()
    for copy in small[2:]:
        copy.wait()
    own_rows = rows_of(HALF * rep_size + me_r)

    for level in range(levels):
        residual = jnp.concatenate([rs_ref[level, t] for t in range(tiles)], axis=0)
        if level > 0:
            for j, step in peers:
                await_val(level - 1, j, step)
            arrived = val_recv[level - 1]
            folded = arrived[:, width:]
            whole = jnp.dot(
                unpack[level - 1, 0], arrived[:, :width], preferred_element_type=F32
            )
            low = jnp.dot(unpack[level - 1, 1], folded, preferred_element_type=F32)
            high = jnp.dot(
                unpack[level - 1, 2], folded[:, : width - fold], preferred_element_type=F32
            )
            residual = residual - (whole + jnp.concatenate([low, high], axis=1))
        load_diag(level).wait()
        solved = solve(level, residual)
        if level + 1 < levels:
            rounded = solved.astype(BF16)
            solved_send[level, tile_span] = rounded
        if level == 0:
            for part in range(panels // chunk):
                load_panel(0, part).start()
            pl.semaphore_wait(barrier, len(peers))
        for step in far_first if level + 1 < levels else ():
            send_solved(level, step).start()
        for t in range(tiles):
            out_ref[level, t] = solved[t * cols : (t + 1) * cols]
        if level + 1 == levels:
            break
        solved_recv[level, me_r, tile_span] = rounded
        if level == 0:
            for j, step in peers:
                send_id(j, step).start()
        for step in range(1, rep_size):
            await_solved(level, step)
        gathered = jnp.dot(
            regroup_ref[...],
            solved_recv[level].reshape(rep_size * group_rows, width),
            preferred_element_type=F32,
        ).astype(BF16)
        store[level * tiles : (level + 1) * tiles] = gathered.reshape(tiles, rhs, width)
        for part in range(panels // chunk):
            load_panel(level, part).wait()
            for p in range(part * chunk, (part + 1) * chunk):
                source = store[src_ref[level, p]]
                product = jnp.dot(source, panel[level, p], preferred_element_type=F32)
                contrib[p * rhs : (p + 1) * rhs] = product.astype(BF16)
        packed = jnp.dot(pack[level], contrib[...], preferred_element_type=F32)
        top, tail = packed[: senders * half], packed[senders * half :]
        is_low = lax.rem(lax.broadcasted_iota(jnp.int32, (senders * half, width - fold), 0), half) < cols
        mixed = jnp.where(is_low, tail[:, : width - fold], tail[:, fold:])
        val_send[level, :, :width] = top.astype(BF16)
        val_send[level, :, width : 2 * width - fold] = mixed.astype(BF16)
        val_send[level, :, 2 * width - fold :] = tail[:, width - fold : fold].astype(BF16)
        for j, step in peers:
            send_val(level, j, step).start()
        val_recv[level, own_rows] = val_send[level, own_rows]
        load_diag(level + 1).start()
        if level + 2 < levels:
            for part in range(panels // chunk):
                load_panel(level + 1, part).start()
        if level == 0:
            learn_ids()

    for j, step in peers:
        send_id(j, step).wait_send()
        for level in range(levels - 1):
            send_val(level, j, step).wait_send()
    for step in range(1, rep_size):
        for level in range(levels - 1):
            send_solved(level, step).wait_send()


def per_device(right_sides, diag_inverse, panel_mats, panel_src, panel_dst):
    levels, tiles, cols, width = right_sides.shape
    panels = panel_mats.shape[1]
    dom_size = lax.axis_size("dom")
    rep_size = lax.axis_size("rep")
    rhs = rep_size * cols
    tile_rows = tiles * cols
    half = 2 * cols
    group_rows = round_up(tile_rows, 16)
    senders = HOOD * rep_size
    chunk = 4 if panels % 4 == 0 else 1
    assert (levels - 1) * 2 * half <= 128 and width % 384 == 0 and half == 8
    dims = (
        levels, tiles, cols, width, panels, dom_size, rep_size, group_rows, chunk
    )
    lanes = jnp.asarray(lane_tables(rep_size, panels, cols))
    regroup = jnp.asarray(regroup_table(rep_size, tiles, cols, group_rows), BF16)
    vmem = pl.BlockSpec(memory_space=pltpu.VMEM)
    hbm = pl.BlockSpec(memory_space=pl.ANY)
    dma = pltpu.SemaphoreType.DMA
    return pl.pallas_call(
        functools.partial(kernel, dims),
        out_shape=jax.ShapeDtypeStruct(right_sides.shape, F32),
        in_specs=[hbm] * 7,
        out_specs=vmem,
        scratch_shapes=[
            pltpu.SMEM(panel_src.shape, jnp.int32),
            pltpu.VMEM(panel_dst.shape, jnp.int32),
            pltpu.VMEM(right_sides.shape, F32),
            pltpu.VMEM(lanes.shape, F32),
            pltpu.VMEM(regroup.shape, BF16),
            dma((5,)),
            pltpu.VMEM(diag_inverse.shape, BF16),
            pltpu.VMEM(panel_mats.shape, BF16),
            pltpu.VMEM(((levels - 1) * tiles, rhs, width), BF16),
            pltpu.VMEM((panels * rhs, width), BF16),
            pltpu.VMEM((levels - 1, 2 * senders * half, panels * rhs), BF16),
            pltpu.VMEM((levels - 1, 3, tile_rows, senders * half), BF16),
            pltpu.VMEM((levels - 1, group_rows, width), BF16),
            pltpu.VMEM((levels - 1, rep_size, group_rows, width), BF16),
            pltpu.VMEM((levels - 1, senders * half, width + width // 3 * 2), BF16),
            pltpu.VMEM((levels - 1, senders * half, width + width // 3 * 2), BF16),
            pltpu.VMEM((HOOD, 1, 128), jnp.int32),
            pltpu.VMEM((senders, 1, 128), jnp.int32),
            dma((levels,)),
            dma((levels - 1, panels // chunk)),
            dma((levels - 1, rep_size)),
            dma((levels - 1, rep_size)),
            dma((levels - 1, senders)),
            dma((levels - 1, senders)),
            dma((senders,)),
            dma((senders,)),
        ],
        compiler_params=pltpu.CompilerParams(
            collective_id=0, has_side_effects=True, vmem_limit_bytes=67043328
        ),
    )(
        panel_src,
        panel_dst,
        right_sides,
        lanes,
        regroup,
        diag_inverse,
        panel_mats,
    )


def solution(mesh):
    return jax.shard_map(
        per_device,
        mesh=mesh,
        in_specs=(
            P(None, "dom", "rep", None),
            P(None, "dom", None, None),
            P(None, ("dom", "rep"), None, None),
            P(None, ("dom", "rep")),
            P(None, ("dom", "rep")),
        ),
        out_specs=P(None, "dom", "rep", None),
        check_vma=False,
    )
```

profile of v0, /device:TPU:0, one launch (start us, length us, event | category | flops | bytes accessed | tf_op | source)
XLA Modules:
  0.0 47.8 jit_solution(10761542073704610813)
XLA Ops:
  0.0 46.2 %shard_map.73 = f32[4,6,4,384]{3,2,1,0:T(4,128)} custom-call(s32[3,16]{1,0:T(4,128)} %src_hbm.1, s32[3,16]{1,0:T(4,128)} %dst_hbm.1, f32[4,6,4,384]{3,2,1,0:T(4,128)} %rs_hbm.1, f32[8,256]{1,0:T(8,128)} %constant.4.clone.lanes_hbm, bf16[96,128]{1,0:T(8,128)(2,1)} %constant.5.clone.regroup_hbm, bf16[4,6,384,384]{3,2,1,0:T(8,128)(2,1)} %diag_hbm.1, ...), custom_call_target="tpu_custom_call" | custom-call | tf_op jit(solution)/shard_map/pallas_call | solution.py:369
  46.2 1.6 %copy.9 = f32[4,6,4,384]{3,2,1,0:T(4,128)} copy(f32[4,6,4,384]{3,2,1,0:T(4,128)} %shard_map.73) | data formatting | bytes 294912
where the time goes:
time: 47.9 us; the launch traced here: 47.8 us
  Pallas kernels  46.2 us (96%)
  local copies, waits for them, and re-layouts  1.59 us (3%)
    pallas_call x1, Pallas kernels, per_device(): pl.pallas_call(functools.partial(kernel, dims), out_shape=jax.ShapeDtypeS...  46.2 us
    unnamed x1, local copies, waits for them, and re-layouts  1.59 us

commit v1 on v0

v1 whole, which is shorter than its diff:
```python
import functools

import jax
import jax.numpy as jnp
from jax import lax
from jax.experimental import pallas as pl
from jax.experimental.pallas import tpu as pltpu
from jax.sharding import PartitionSpec as P

HALF = 2
SLOTS = 3
HOOD = 2 * HALF + 2
MESH = pl.DeviceIdType.MESH
F32 = jnp.float32
BF16 = jnp.bfloat16


def iota(shape, dim):
    return lax.broadcasted_iota(jnp.int32, shape, dim).astype(F32)


def div(value, unit):
    return jnp.floor((value + 0.5) * (1.0 / unit))


def kernel(
    dims,
    src_hbm, dst_hbm, rs_hbm, diag_hbm, panel_hbm,
    out_ref,
    src_ref, dst_ref, rs_ref, small_sem,
    diag, panels_by_level, store, solved_ref, placed,
    slots_v, slots_s, slot_sem,
    val_send, val_recv, unpack, part_send, part_recv, id_send, id_recv,
    diag_sem, panel_sem, val_ssem, val_rsem, part_ssem, part_rsem, id_ssem, id_rsem,
):
    levels, tiles, cols, width, panels, dom_size, rep_size, chunk = dims
    far = dom_size // 2
    block = rep_size // 2 * cols
    tile_rows = tiles * block
    rows = SLOTS * block
    pairs = 2 * HOOD
    zero_tile = (levels - 1) * tiles
    me_d = lax.axis_index("dom")
    me_r = lax.axis_index("rep")
    my_half = lax.rem(me_r, 2)
    my_place = me_r // 2
    partner = me_r + 1 - 2 * my_half
    offsets = [o - HALF for o in range(HOOD - 1)] + [far]
    order = (HOOD - 1, 0, HOOD - 2, HALF, 1, HOOD - 3)

    def peer_dom(offset):
        return lax.rem(me_d + (offset + dom_size), dom_size)

    def peer_rep(step):
        return lax.rem(me_r + step, rep_size)

    peers = [(j, side) for j in order for side in (1, 0) if (offsets[j], side) != (0, 0)]
    others = [s for s in range(2, rep_size)] + [1]

    def load_diag(level):
        return pltpu.make_async_copy(diag_hbm.at[level], diag.at[level], diag_sem.at[level])

    def load_panel(level, part):
        span = pl.ds(part * chunk, chunk)
        return pltpu.make_async_copy(
            panel_hbm.at[level, span], panels_by_level[level].at[span], panel_sem.at[level, part]
        )

    def side_rep(side):
        return partner if side else me_r

    def side_half(side):
        return 1 - my_half if side else my_half

    def send_id(j, side):
        return pltpu.make_async_remote_copy(
            src_ref=id_send.at[j],
            dst_ref=id_recv.at[j, my_half],
            send_sem=id_ssem.at[j, side],
            recv_sem=id_rsem.at[j, my_half],
            device_id=(peer_dom(offsets[j]), side_rep(side)),
            device_id_type=MESH,
        )

    def await_id(j, side):
        pltpu.make_async_remote_copy(
            src_ref=id_send.at[j],
            dst_ref=id_recv.at[j, side_half(side)],
            send_sem=id_ssem.at[j, side],
            recv_sem=id_rsem.at[j, side_half(side)],
            device_id=(peer_dom(-offsets[j]), side_rep(side)),
            device_id_type=MESH,
        ).wait_recv()

    def send_val(level, j, side):
        return pltpu.make_async_remote_copy(
            src_ref=val_send.at[level, side_half(side), j],
            dst_ref=val_recv.at[level, j, my_half],
            send_sem=val_ssem.at[level, j, side],
            recv_sem=val_rsem.at[level, j, my_half],
            device_id=(peer_dom(offsets[j]), side_rep(side)),
            device_id_type=MESH,
        )

    def await_val(level, j, side):
        pltpu.make_async_remote_copy(
            src_ref=val_send.at[level, side_half(side), j],
            dst_ref=val_recv.at[level, j, side_half(side)],
            send_sem=val_ssem.at[level, j, side],
            recv_sem=val_rsem.at[level, j, side_half(side)],
            device_id=(peer_dom(-offsets[j]), side_rep(side)),
            device_id_type=MESH,
        ).wait_recv()

    def send_part(level, step):
        return pltpu.make_async_remote_copy(
            src_ref=part_send.at[level],
            dst_ref=part_recv.at[level, me_r],
            send_sem=part_ssem.at[level, step],
            recv_sem=part_rsem.at[level, me_r],
            device_id=(me_d, peer_rep(step)),
            device_id_type=MESH,
        )

    def await_part(level, step):
        slot = peer_rep(step)
        pltpu.make_async_remote_copy(
            src_ref=part_send.at[level],
            dst_ref=part_recv.at[level, slot],
            send_sem=part_ssem.at[level, step],
            recv_sem=part_rsem.at[level, slot],
            device_id=(me_d, slot),
            device_id_type=MESH,
        ).wait_recv()

    small = [
        pltpu.make_async_copy(hbm, ref, small_sem.at[i])
        for i, (hbm, ref) in enumerate(((rs_hbm, rs_ref), (dst_hbm, dst_ref), (src_hbm, src_ref)))
    ]
    for copy in small:
        copy.start()
    load_diag(0).start()
    for part in range(panels // chunk):
        load_panel(0, part).start()

    barrier = pltpu.get_barrier_semaphore()
    for j, side in peers:
        pl.semaphore_signal(
            barrier,
            inc=1,
            device_id=(peer_dom(offsets[j]), side_rep(side)),
            device_id_type=MESH,
        )
    for step in others:
        pl.semaphore_signal(
            barrier, inc=1, device_id=(me_d, peer_rep(step)), device_id_type=MESH
        )

    def place(level):
        row = lax.broadcasted_iota(jnp.int32, (block, width), 0) // cols
        for t in range(tiles):
            twice = jnp.concatenate([rs_ref[level, t]] * (rep_size // 2), axis=0)
            placed[level, t * block : (t + 1) * block] = jnp.where(row == my_place, twice, 0.0)

    def share(level, partial):
        rounded = partial.astype(BF16)
        part_send[level] = rounded
        return rounded

    def route():
        owner = me_d.astype(F32)
        row16 = iota((panels, panels), 0)
        col16 = iota((panels, panels), 1)
        lane = iota((1, 128), 1)
        id_level = div(lane, rows)
        id_rest = lane - rows * id_level
        id_slot = div(id_rest, block)
        id_col = id_rest - block * id_slot
        panel_col = iota((panels, 1), 0)
        wanted = [jnp.zeros((1, 128), F32) for _ in range(HOOD)]
        for l in range(levels - 1):
            drow = dst_ref[l : l + 1, :].astype(F32)
            srow = src_ref[l : l + 1, :].astype(F32)
            dcol = jnp.sum(jnp.where(row16 == col16, drow, 0.0), axis=1, keepdims=True)
            scol = jnp.sum(jnp.where(row16 == col16, srow, 0.0), axis=1, keepdims=True)
            trow = jnp.where(drow >= 0, div(drow, tiles), -1.0)
            tcol = jnp.where(dcol >= 0, div(dcol, tiles), -1.0)
            earlier = (tcol == trow) & (drow >= 0) & (col16 < row16)
            rank = jnp.sum(jnp.where(earlier, 1.0, 0.0), axis=1, keepdims=True)
            away = tcol - owner
            away = away + jnp.where(away < 0, float(dom_size), 0.0)
            near = away + HALF
            near = near - jnp.where(near >= dom_size, float(dom_size), 0.0)
            reach = jnp.where(away == far, float(HOOD - 1), near)
            reach = jnp.where(dcol >= 0, reach, -1.0)
            spot = jnp.where(dcol >= 0, reach * SLOTS + rank, -1.0)
            tile = dcol - tiles * tcol
            here = spot == lane
            which = jnp.sum(jnp.where(here, panel_col, 0.0), axis=0, keepdims=True)
            source = jnp.sum(jnp.where(here, scol - zero_tile, 0.0), axis=0, keepdims=True)
            slots_v[2 * l : 2 * l + 1, :] = which.astype(jnp.int32)
            slots_v[2 * l + 1 : 2 * l + 2, :] = (source + zero_tile).astype(jnp.int32)
            mine = (rank == id_slot) & (id_level == l)
            for j in range(HOOD):
                found = jnp.where(mine & (reach == j), tile + 1.0, 0.0)
                wanted[j] = wanted[j] + jnp.sum(found, axis=0, keepdims=True)
        for j in range(HOOD):
            row = jnp.where(wanted[j] > 0, (wanted[j] - 1.0) * block + id_col, -1.0)
            id_send[j] = row.astype(jnp.int32)
        id_recv[HALF, my_half] = id_send[HALF]

    def learn_ids():
        for j, side in peers:
            await_id(j, side)
        row_of = iota((pairs, 128), 0)
        ids = jnp.zeros((pairs, 128), F32)
        for j in range(HOOD):
            for h in range(2):
                ids = jnp.where(row_of == 2 * j + h, id_recv[j, h].astype(F32), ids)
        ids = ids.astype(BF16)
        span = pairs * rows
        lane = iota((1, span), 1)
        lane_sender = div(lane, rows)
        lane_in = lane - rows * lane_sender
        for l in range(levels - 1):
            take = jnp.where(iota((128, span), 0) == lane_in + l * rows, 1.0, 0.0)
            every = jnp.dot(ids, take.astype(BF16), preferred_element_type=F32)
            own = jnp.where(iota((pairs, span), 0) == lane_sender, every, 0.0)
            goal = jnp.sum(own, axis=0, keepdims=True)
            unpack[l] = jnp.where(iota((tile_rows, span), 0) == goal, 1.0, 0.0).astype(BF16)

    def emit(level):
        for t in range(tiles):
            mine = solved_ref[level, t, my_half]
            picked = mine[:cols]
            for q in range(1, rep_size // 2):
                picked = jnp.where(my_place == q, mine[q * cols : (q + 1) * cols], picked)
            out_ref[level, t] = picked

    small[0].wait()
    place(0)
    rounded = share(0, placed[0])
    pl.semaphore_wait(barrier, len(peers) + len(others))
    for step in others:
        send_part(0, step).start()
    part_recv[0, me_r] = rounded
    small[1].wait()
    small[2].wait()
    route()
    slot_copy = pltpu.make_async_copy(slots_v, slots_s, slot_sem)
    slot_copy.start()
    for j, side in peers:
        send_id(j, side).start()
    for level in range(1, levels):
        place(level)
    store[zero_tile] = jnp.zeros((2 * block, width), BF16)

    for level in range(levels):
        for step in others:
            await_part(level, step)
        halves = []
        for h in range(2):
            total = part_recv[level, h].astype(F32)
            for r in range(h + 2, rep_size, 2):
                total = total + part_recv[level, r].astype(F32)
            halves.append(total)
        load_diag(level).wait()
        for t in range(tiles):
            span = slice(t * block, (t + 1) * block)
            residual = jnp.concatenate([half[span] for half in halves], axis=0).astype(BF16)
            solved = jnp.dot(residual, diag[level, t], preferred_element_type=F32)
            if level + 1 < levels:
                store[level * tiles + t] = solved.astype(BF16)
            for h in range(2):
                solved_ref[level, t, h] = solved[h * block : (h + 1) * block]
        if level + 1 == levels:
            break
        if level == 0:
            slot_copy.wait()
        for part in range(panels // chunk):
            load_panel(level, part).wait()
        for j in order:
            for k in range(SLOTS):
                which = jnp.clip(slots_s[2 * level, j * SLOTS + k], 0, panels - 1)
                source = jnp.clip(slots_s[2 * level + 1, j * SLOTS + k], 0, zero_tile)
                product = jnp.dot(
                    store[source], panels_by_level[level][which], preferred_element_type=F32
                ).astype(BF16)
                for h in range(2):
                    val_send[level, h, j, k * block : (k + 1) * block] = product[
                        h * block : (h + 1) * block
                    ]
            for side in (1, 0):
                if (j, side) in peers:
                    send_val(level, j, side).start()
        val_recv[level, HALF, my_half] = val_send[level, my_half, HALF]
        load_diag(level + 1).start()
        if level + 2 < levels:
            for part in range(panels // chunk):
                load_panel(level + 1, part).start()
        if level == 0:
            learn_ids()
        emit(level)
        for j, side in peers:
            await_val(level, j, side)
        arrived = val_recv[level].reshape(pairs * rows, width)
        incoming = jnp.dot(unpack[level], arrived, preferred_element_type=F32)
        rounded = share(level + 1, placed[level + 1] - incoming)
        for step in others:
            send_part(level + 1, step).start()
        part_recv[level + 1, me_r] = rounded

    emit(levels - 1)
    for j, side in peers:
        send_id(j, side).wait_send()
        for level in range(levels - 1):
            send_val(level, j, side).wait_send()
    for step in others:
        for level in range(levels):
            send_part(level, step).wait_send()


def per_device(right_sides, diag_inverse, panel_mats, panel_src, panel_dst):
    levels, tiles, cols, width = right_sides.shape
    panels = panel_mats.shape[1]
    dom_size = lax.axis_size("dom")
    rep_size = lax.axis_size("rep")
    block = rep_size // 2 * cols
    tile_rows = tiles * block
    rows = SLOTS * block
    chunk = 4 if panels % 4 == 0 else 1
    assert rep_size % 2 == 0 and block % 8 == 0 and (levels - 1) * rows <= 128
    dims = (levels, tiles, cols, width, panels, dom_size, rep_size, chunk)
    vmem = pl.BlockSpec(memory_space=pltpu.VMEM)
    hbm = pl.BlockSpec(memory_space=pl.ANY)
    dma = pltpu.SemaphoreType.DMA
    i32 = jnp.int32
    return pl.pallas_call(
        functools.partial(kernel, dims),
        out_shape=jax.ShapeDtypeStruct(right_sides.shape, F32),
        in_specs=[hbm] * 5,
        out_specs=vmem,
        scratch_shapes=[
            pltpu.VMEM(panel_src.shape, i32),
            pltpu.VMEM(panel_dst.shape, i32),
            pltpu.VMEM(right_sides.shape, F32),
            dma((3,)),
            pltpu.VMEM(diag_inverse.shape, BF16),
            [pltpu.VMEM(panel_mats.shape[1:], BF16) for _ in range(levels - 1)],
            pltpu.VMEM(((levels - 1) * tiles + 1, 2 * block, width), BF16),
            pltpu.VMEM((levels, tiles, 2, block, width), F32),
            pltpu.VMEM((levels, tile_rows, width), F32),
            pltpu.VMEM((8, 128), i32),
            pltpu.SMEM((8, 128), i32),
            dma,
            pltpu.VMEM((levels - 1, 2, HOOD, rows, width), BF16),
            pltpu.VMEM((levels - 1, HOOD, 2, rows, width), BF16),
            pltpu.VMEM((levels - 1, tile_rows, 2 * HOOD * rows), BF16),
            pltpu.VMEM((levels, tile_rows, width), BF16),
            pltpu.VMEM((levels, rep_size, tile_rows, width), BF16),
            pltpu.VMEM((HOOD, 1, 128), i32),
            pltpu.VMEM((HOOD, 2, 1, 128), i32),
            dma((levels,)),
            dma((levels - 1, panels // chunk)),
            dma((levels - 1, HOOD, 2)),
            dma((levels - 1, HOOD, 2)),
            dma((levels, rep_size)),
            dma((levels, rep_size)),
            dma((HOOD, 2)),
            dma((HOOD, 2)),
        ],
        compiler_params=pltpu.CompilerParams(
            collective_id=0, has_side_effects=True, vmem_limit_bytes=67043328
        ),
    )(panel_src, panel_dst, right_sides, diag_inverse, panel_mats)


def solution(mesh):
    return jax.shard_map(
        per_device,
        mesh=mesh,
        in_specs=(
            P(None, "dom", "rep", None),
            P(None, "dom", None, None),
            P(None, ("dom", "rep"), None, None),
            P(None, ("dom", "rep")),
            P(None, ("dom", "rep")),
        ),
        out_specs=P(None, "dom", "rep", None),
        check_vma=False,
    )
```

time: 47.9 us -> 45.4 us (0.948)
  Pallas kernels: 46.2 us -> 43.7 us
    pallas_call x1, Pallas kernels: 46.2 us -> 43.7 us  [per_device(): pl.pallas_call(functools.partial(kernel, dims), out_shape=jax.ShapeDtypeS...]
where the time goes in v1:
time: 45.4 us; the launch traced here: 45.3 us
  Pallas kernels  43.7 us (96%)
  local copies, waits for them, and re-layouts  1.59 us (4%)
    pallas_call x1, Pallas kernels, per_device(): pl.pallas_call(functools.partial(kernel, dims), out_shape=jax.ShapeDtypeS...  43.7 us
    unnamed x1, local copies, waits for them, and re-layouts  1.59 us

profile of v1, /device:TPU:0, one launch (start us, length us, event | category | flops | bytes accessed | tf_op | source)
XLA Modules:
  0.0 45.3 jit_solution(6022977143637746678)
XLA Ops:
  0.0 43.7 %shard_map.55 = f32[4,6,4,384]{3,2,1,0:T(4,128)} custom-call(s32[3,16]{1,0:T(4,128)} %src_hbm.1, s32[3,16]{1,0:T(4,128)} %dst_hbm.1, f32[4,6,4,384]{3,2,1,0:T(4,128)} %rs_hbm.1, bf16[4,6,384,384]{3,2,1,0:T(8,128)(2,1)} %diag_hbm.1, bf16[3,16,384,384]{3,2,1,0:T(8,128)(2,1)} %panel_hbm.1), custom_call_target="tpu_custom_call" | custom-call | tf_op jit(solution)/shard_map/pallas_call | solution.py:338
  43.7 1.6 %copy.7 = f32[4,6,4,384]{3,2,1,0:T(4,128)} copy(f32[4,6,4,384]{3,2,1,0:T(4,128)} %shard_map.55) | data formatting | bytes 294912

commit v2 on v1

--- a/solution.py
+++ b/solution.py
@@ -31,7 +31,9 @@
     diag, panels_by_level, store, solved_ref, placed,
     slots_v, slots_s, slot_sem,
     val_send, val_recv, unpack, part_send, part_recv, id_send, id_recv,
+    last_send, last_recv, last_unpack,
     diag_sem, panel_sem, val_ssem, val_rsem, part_ssem, part_rsem, id_ssem, id_rsem,
+    last_ssem, last_rsem,
 ):
     levels, tiles, cols, width, panels, dom_size, rep_size, chunk = dims
     far = dom_size // 2
@@ -39,6 +41,11 @@
     tile_rows = tiles * block
     rows = SLOTS * block
     pairs = 2 * HOOD
+    senders = HOOD * rep_size
+    half_rows = 2 * cols
+    third = width // 3
+    own_rows = tiles * cols
+    last = levels - 2
     zero_tile = (levels - 1) * tiles
     me_d = lax.axis_index("dom")
     me_r = lax.axis_index("rep")
@@ -56,6 +63,7 @@
 
     peers = [(j, side) for j in order for side in (1, 0) if (offsets[j], side) != (0, 0)]
     others = [s for s in range(2, rep_size)] + [1]
+    everyone = [(j, step) for j in order for step in others + [0] if (offsets[j], step) != (0, 0)]
 
     def load_diag(level):
         return pltpu.make_async_copy(diag_hbm.at[level], diag.at[level], diag_sem.at[level])
@@ -72,23 +80,45 @@
     def side_half(side):
         return 1 - my_half if side else my_half
 
-    def send_id(j, side):
+    def send_id(j, step):
         return pltpu.make_async_remote_copy(
             src_ref=id_send.at[j],
-            dst_ref=id_recv.at[j, my_half],
-            send_sem=id_ssem.at[j, side],
-            recv_sem=id_rsem.at[j, my_half],
-            device_id=(peer_dom(offsets[j]), side_rep(side)),
-            device_id_type=MESH,
-        )
-
-    def await_id(j, side):
+            dst_ref=id_recv.at[j, me_r],
+            send_sem=id_ssem.at[j, step],
+            recv_sem=id_rsem.at[j, me_r],
+            device_id=(peer_dom(offsets[j]), peer_rep(step)),
+            device_id_type=MESH,
+        )
+
+    def await_id(j, step):
+        slot = peer_rep(step)
         pltpu.make_async_remote_copy(
             src_ref=id_send.at[j],
-            dst_ref=id_recv.at[j, side_half(side)],
-            send_sem=id_ssem.at[j, side],
-            recv_sem=id_rsem.at[j, side_half(side)],
-            device_id=(peer_dom(-offsets[j]), side_rep(side)),
+            dst_ref=id_recv.at[j, slot],
+            send_sem=id_ssem.at[j, step],
+            recv_sem=id_rsem.at[j, slot],
+            device_id=(peer_dom(-offsets[j]), slot),
+            device_id_type=MESH,
+        ).wait_recv()
+
+    def send_last(j, step):
+        return pltpu.make_async_remote_copy(
+            src_ref=last_send.at[j, peer_rep(step)],
+            dst_ref=last_recv.at[j, me_r],
+            send_sem=last_ssem.at[j, step],
+            recv_sem=last_rsem.at[j, me_r],
+            device_id=(peer_dom(offsets[j]), peer_rep(step)),
+            device_id_type=MESH,
+        )
+
+    def await_last(j, step):
+        slot = peer_rep(step)
+        pltpu.make_async_remote_copy(
+            src_ref=last_send.at[j, slot],
+            dst_ref=last_recv.at[j, slot],
+            send_sem=last_ssem.at[j, step],
+            recv_sem=last_rsem.at[j, slot],
+            device_id=(peer_dom(-offsets[j]), slot),
             device_id_type=MESH,
         ).wait_recv()
 
@@ -112,10 +142,13 @@
             device_id_type=MESH,
         ).wait_recv()
 
+    def part_span(level):
+        return pl.ds(0, tile_rows if level else own_rows)
+
     def send_part(level, step):
         return pltpu.make_async_remote_copy(
-            src_ref=part_send.at[level],
-            dst_ref=part_recv.at[level, me_r],
+            src_ref=part_send.at[level, part_span(level)],
+            dst_ref=part_recv.at[level, me_r, part_span(level)],
             send_sem=part_ssem.at[level, step],
             recv_sem=part_rsem.at[level, me_r],
             device_id=(me_d, peer_rep(step)),
@@ -125,8 +158,8 @@
     def await_part(level, step):
         slot = peer_rep(step)
         pltpu.make_async_remote_copy(
-            src_ref=part_send.at[level],
-            dst_ref=part_recv.at[level, slot],
+            src_ref=part_send.at[level, part_span(level)],
+            dst_ref=part_recv.at[level, slot, part_span(level)],
             send_sem=part_ssem.at[level, step],
             recv_sem=part_rsem.at[level, slot],
             device_id=(me_d, slot),
@@ -144,16 +177,12 @@
         load_panel(0, part).start()
 
     barrier = pltpu.get_barrier_semaphore()
-    for j, side in peers:
+    for j, step in everyone:
         pl.semaphore_signal(
             barrier,
             inc=1,
-            device_id=(peer_dom(offsets[j]), side_rep(side)),
-            device_id_type=MESH,
-        )
-    for step in others:
-        pl.semaphore_signal(
-            barrier, inc=1, device_id=(me_d, peer_rep(step)), device_id_type=MESH
+            device_id=(peer_dom(offsets[j]), peer_rep(step)),
+            device_id_type=MESH,
         )
 
     def place(level):
@@ -164,8 +193,10 @@
 
     def share(level, partial):
         rounded = partial.astype(BF16)
-        part_send[level] = rounded
-        return rounded
+        part_send[level, : rounded.shape[0]] = rounded
+        for step in others:
+            send_part(level, step).start()
+        part_recv[level, me_r, : rounded.shape[0]] = rounded
 
     def route():
         owner = me_d.astype(F32)
@@ -200,34 +231,53 @@
             source = jnp.sum(jnp.where(here, scol - zero_tile, 0.0), axis=0, keepdims=True)
             slots_v[2 * l : 2 * l + 1, :] = which.astype(jnp.int32)
             slots_v[2 * l + 1 : 2 * l + 2, :] = (source + zero_tile).astype(jnp.int32)
+            if l == last:
+                id_slot = div(id_rest, cols)
+                id_col = id_rest - cols * id_slot
             mine = (rank == id_slot) & (id_level == l)
             for j in range(HOOD):
-                found = jnp.where(mine & (reach == j), tile + 1.0, 0.0)
+                spread = tile * (cols if l == last else block) + id_col + 1.0
+                found = jnp.where(mine & (reach == j), spread, 0.0)
                 wanted[j] = wanted[j] + jnp.sum(found, axis=0, keepdims=True)
         for j in range(HOOD):
-            row = jnp.where(wanted[j] > 0, (wanted[j] - 1.0) * block + id_col, -1.0)
-            id_send[j] = row.astype(jnp.int32)
-        id_recv[HALF, my_half] = id_send[HALF]
+            id_send[j] = (wanted[j] - 1.0).astype(jnp.int32)
+        id_recv[HALF, me_r] = id_send[HALF]
 
     def learn_ids():
-        for j, side in peers:
-            await_id(j, side)
-        row_of = iota((pairs, 128), 0)
-        ids = jnp.zeros((pairs, 128), F32)
+        for j, step in everyone:
+            await_id(j, step)
+
+        def lookup(ids, count, span, lane_in):
+            lane_sender = div(iota((1, span), 1), span // count)
+            take = jnp.where(iota((128, span), 0) == lane_in, 1.0, 0.0)
+            every = jnp.dot(ids, take.astype(BF16), preferred_element_type=F32)
+            own = jnp.where(iota((count, span), 0) == lane_sender, every, 0.0)
+            return jnp.sum(own, axis=0, keepdims=True)
+
+        near = jnp.zeros((pairs, 128), F32)
+        full = jnp.zeros((senders, 128), F32)
         for j in range(HOOD):
-            for h in range(2):
-                ids = jnp.where(row_of == 2 * j + h, id_recv[j, h].astype(F32), ids)
-        ids = ids.astype(BF16)
+            for side in range(2):
+                row = id_recv[j, my_place * 2 + side].astype(F32)
+                near = jnp.where(iota((pairs, 128), 0) == 2 * j + side, row, near)
+            for r in range(rep_size):
+                row = id_recv[j, r].astype(F32)
+                full = jnp.where(iota((senders, 128), 0) == rep_size * j + r, row, full)
         span = pairs * rows
         lane = iota((1, span), 1)
-        lane_sender = div(lane, rows)
-        lane_in = lane - rows * lane_sender
-        for l in range(levels - 1):
-            take = jnp.where(iota((128, span), 0) == lane_in + l * rows, 1.0, 0.0)
-            every = jnp.dot(ids, take.astype(BF16), preferred_element_type=F32)
-            own = jnp.where(iota((pairs, span), 0) == lane_sender, every, 0.0)
-            goal = jnp.sum(own, axis=0, keepdims=True)
+        lane_in = lane - rows * div(lane, rows)
+        for l in range(last):
+            goal = lookup(near.astype(BF16), pairs, span, lane_in + l * rows)
             unpack[l] = jnp.where(iota((tile_rows, span), 0) == goal, 1.0, 0.0).astype(BF16)
+        span = senders * half_rows
+        lane = iota((1, span), 1)
+        lane_in = lane - half_rows * div(lane, half_rows)
+        low = lane_in < cols
+        full = full.astype(BF16)
+        first = lookup(full, senders, span, lane_in + last * rows)
+        fold = lookup(full, senders, span, lane_in + last * rows + jnp.where(low, 2.0 * cols, 1.0 * cols))
+        for i, goal in enumerate((first, jnp.where(low, fold, -1.0), jnp.where(low, -1.0, fold))):
+            last_unpack[i] = jnp.where(iota((own_rows, span), 0) == goal, 1.0, 0.0).astype(BF16)
 
     def emit(level):
         for t in range(tiles):
@@ -237,86 +287,134 @@
                 picked = jnp.where(my_place == q, mine[q * cols : (q + 1) * cols], picked)
             out_ref[level, t] = picked
 
+    def own_sides(level):
+        return jnp.concatenate([rs_ref[level, t] for t in range(tiles)], axis=0)
+
     small[0].wait()
-    place(0)
-    rounded = share(0, placed[0])
-    pl.semaphore_wait(barrier, len(peers) + len(others))
-    for step in others:
-        send_part(0, step).start()
-    part_recv[0, me_r] = rounded
+    pl.semaphore_wait(barrier, len(everyone))
+    share(0, own_sides(0))
     small[1].wait()
     small[2].wait()
     route()
     slot_copy = pltpu.make_async_copy(slots_v, slots_s, slot_sem)
     slot_copy.start()
-    for j, side in peers:
-        send_id(j, side).start()
-    for level in range(1, levels):
+    for j, step in everyone:
+        send_id(j, step).start()
+    for level in range(1, levels - 1):
         place(level)
     store[zero_tile] = jnp.zeros((2 * block, width), BF16)
 
-    for level in range(levels):
+    for level in range(levels - 1):
         for step in others:
             await_part(level, step)
-        halves = []
-        for h in range(2):
-            total = part_recv[level, h].astype(F32)
-            for r in range(h + 2, rep_size, 2):
-                total = total + part_recv[level, r].astype(F32)
-            halves.append(total)
+        if level == 0:
+            parts = [part_recv[0, r, :own_rows].astype(F32) for r in range(rep_size)]
+            residuals = [
+                jnp.concatenate(
+                    [
+                        parts[r][t * cols : (t + 1) * cols]
+                        for h in range(2)
+                        for r in range(h, rep_size, 2)
+                    ],
+                    axis=0,
+                )
+                for t in range(tiles)
+            ]
+        else:
+            halves = []
+            for h in range(2):
+                total = part_recv[level, h].astype(F32)
+                for r in range(h + 2, rep_size, 2):
+                    total = total + part_recv[level, r].astype(F32)
+                halves.append(total)
+            residuals = [
+                jnp.concatenate([half[t * block : (t + 1) * block] for half in halves], axis=0)
+                for t in range(tiles)
+            ]
         load_diag(level).wait()
         for t in range(tiles):
-            span = slice(t * block, (t + 1) * block)
-            residual = jnp.concatenate([half[span] for half in halves], axis=0).astype(BF16)
+            residual = residuals[t].astype(BF16)
             solved = jnp.dot(residual, diag[level, t], preferred_element_type=F32)
-            if level + 1 < levels:
-                store[level * tiles + t] = solved.astype(BF16)
+            store[level * tiles + t] = solved.astype(BF16)
             for h in range(2):
                 solved_ref[level, t, h] = solved[h * block : (h + 1) * block]
-        if level + 1 == levels:
-            break
         if level == 0:
             slot_copy.wait()
         for part in range(panels // chunk):
             load_panel(level, part).wait()
         for j in order:
+            products = []
             for k in range(SLOTS):
                 which = jnp.clip(slots_s[2 * level, j * SLOTS + k], 0, panels - 1)
                 source = jnp.clip(slots_s[2 * level + 1, j * SLOTS + k], 0, zero_tile)
-                product = jnp.dot(
-                    store[source], panels_by_level[level][which], preferred_element_type=F32
-                ).astype(BF16)
-                for h in range(2):
-                    val_send[level, h, j, k * block : (k + 1) * block] = product[
-                        h * block : (h + 1) * block
-                    ]
-            for side in (1, 0):
-                if (j, side) in peers:
-                    send_val(level, j, side).start()
-        val_recv[level, HALF, my_half] = val_send[level, my_half, HALF]
+                products.append(
+                    jnp.dot(
+                        store[source], panels_by_level[level][which], preferred_element_type=F32
+                    )
+                )
+            if level < last:
+                for k in range(SLOTS):
+                    rounded = products[k].astype(BF16)
+                    for h in range(2):
+                        val_send[level, h, j, k * block : (k + 1) * block] = rounded[
+                            h * block : (h + 1) * block
+                        ]
+                for side in (1, 0):
+                    if (j, side) in peers:
+                        send_val(level, j, side).start()
+            else:
+                for r in range(rep_size):
+                    begin = r % 2 * block + r // 2 * cols
+                    piece = [p[begin : begin + cols] for p in products]
+                    last_send[j, r, :, :width] = jnp.concatenate(piece[:2], axis=0).astype(BF16)
+                    tail = piece[2]
+                    mixed = jnp.concatenate([tail[:, :third], tail[:, 2 * third :]], axis=0)
+                    again = jnp.concatenate([tail[:, third : 2 * third]] * 2, axis=0)
+                    last_send[j, r, :, width : width + third] = mixed.astype(BF16)
+                    last_send[j, r, :, width + third :] = again.astype(BF16)
+                for step in others + [0]:
+                    if (j, step) in everyone:
+                        send_last(j, step).start()
+        if level < last:
+            val_recv[level, HALF, my_half] = val_send[level, my_half, HALF]
+        else:
+            last_recv[HALF, me_r] = last_send[HALF, me_r]
         load_diag(level + 1).start()
-        if level + 2 < levels:
+        if level < last:
             for part in range(panels // chunk):
                 load_panel(level + 1, part).start()
         if level == 0:
             learn_ids()
         emit(level)
-        for j, side in peers:
-            await_val(level, j, side)
-        arrived = val_recv[level].reshape(pairs * rows, width)
-        incoming = jnp.dot(unpack[level], arrived, preferred_element_type=F32)
-        rounded = share(level + 1, placed[level + 1] - incoming)
-        for step in others:
-            send_part(level + 1, step).start()
-        part_recv[level + 1, me_r] = rounded
-
-    emit(levels - 1)
+        if level < last:
+            for j, side in peers:
+                await_val(level, j, side)
+            arrived = val_recv[level].reshape(pairs * rows, width)
+            incoming = jnp.dot(unpack[level], arrived, preferred_element_type=F32)
+            share(level + 1, placed[level + 1] - incoming)
+
+    for j, step in everyone:
+        await_last(j, step)
+    arrived = last_recv[...].reshape(senders * half_rows, width + 2 * third)
+    folded = arrived[:, width:]
+    whole = jnp.dot(last_unpack[0], arrived[:, :width], preferred_element_type=F32)
+    low = jnp.dot(last_unpack[1], folded, preferred_element_type=F32)
+    high = jnp.dot(last_unpack[2], folded[:, :third], preferred_element_type=F32)
+    residual = own_sides(levels - 1) - (whole + jnp.concatenate([low, high], axis=1))
+    residual = residual.astype(BF16)
+    load_diag(levels - 1).wait()
+    for t in range(tiles):
+        solved = jnp.dot(residual, diag[levels - 1, t], preferred_element_type=F32)
+        out_ref[levels - 1, t] = solved[t * cols : (t + 1) * cols]
+
+    for j, step in everyone:
+        send_id(j, step).wait_send()
+        send_last(j, step).wait_send()
     for j, side in peers:
-        send_id(j, side).wait_send()
-        for level in range(levels - 1):
+        for level in range(last):
             send_val(level, j, side).wait_send()
     for step in others:
-        for level in range(levels):
+        for level in range(levels - 1):
             send_part(level, step).wait_send()
 
 
@@ -330,6 +428,7 @@
     rows = SLOTS * block
     chunk = 4 if panels % 4 == 0 else 1
     assert rep_size % 2 == 0 and block % 8 == 0 and (levels - 1) * rows <= 128
+    assert 2 * cols == 8 and width % 384 == 0 and levels > 2
     dims = (levels, tiles, cols, width, panels, dom_size, rep_size, chunk)
     vmem = pl.BlockSpec(memory_space=pltpu.VMEM)
     hbm = pl.BlockSpec(memory_space=pl.ANY)
@@ -348,26 +447,31 @@
             pltpu.VMEM(diag_inverse.shape, BF16),
             [pltpu.VMEM(panel_mats.shape[1:], BF16) for _ in range(levels - 1)],
             pltpu.VMEM(((levels - 1) * tiles + 1, 2 * block, width), BF16),
-            pltpu.VMEM((levels, tiles, 2, block, width), F32),
-            pltpu.VMEM((levels, tile_rows, width), F32),
+            pltpu.VMEM((levels - 1, tiles, 2, block, width), F32),
+            pltpu.VMEM((levels - 1, tile_rows, width), F32),
             pltpu.VMEM((8, 128), i32),
             pltpu.SMEM((8, 128), i32),
             dma,
-            pltpu.VMEM((levels - 1, 2, HOOD, rows, width), BF16),
-            pltpu.VMEM((levels - 1, HOOD, 2, rows, width), BF16),
-            pltpu.VMEM((levels - 1, tile_rows, 2 * HOOD * rows), BF16),
-            pltpu.VMEM((levels, tile_rows, width), BF16),
-            pltpu.VMEM((levels, rep_size, tile_rows, width), BF16),
+            pltpu.VMEM((levels - 2, 2, HOOD, rows, width), BF16),
+            pltpu.VMEM((levels - 2, HOOD, 2, rows, width), BF16),
+            pltpu.VMEM((levels - 2, tile_rows, 2 * HOOD * rows), BF16),
+            pltpu.VMEM((levels - 1, tile_rows, width), BF16),
+            pltpu.VMEM((levels - 1, rep_size, tile_rows, width), BF16),
             pltpu.VMEM((HOOD, 1, 128), i32),
-            pltpu.VMEM((HOOD, 2, 1, 128), i32),
+            pltpu.VMEM((HOOD, rep_size, 1, 128), i32),
+            pltpu.VMEM((HOOD, rep_size, 2 * cols, width + width // 3 * 2), BF16),
+            pltpu.VMEM((HOOD, rep_size, 2 * cols, width + width // 3 * 2), BF16),
+            pltpu.VMEM((3, tiles * cols, HOOD * rep_size * 2 * cols), BF16),
             dma((levels,)),
             dma((levels - 1, panels // chunk)),
-            dma((levels - 1, HOOD, 2)),
-            dma((levels - 1, HOOD, 2)),
-            dma((levels, rep_size)),
-            dma((levels, rep_size)),
-            dma((HOOD, 2)),
-            dma((HOOD, 2)),
+            dma((levels - 2, HOOD, 2)),
+            dma((levels - 2, HOOD, 2)),
+            dma((levels - 1, rep_size)),
+            dma((levels - 1, rep_size)),
+            dma((HOOD, rep_size)),
+            dma((HOOD, rep_size)),
+            dma((HOOD, rep_size)),
+            dma((HOOD, rep_size)),
         ],
         compiler_params=pltpu.CompilerParams(
             collective_id=0, has_side_effects=True, vmem_limit_bytes=67043328

time: 45.4 us -> 44 us (0.969)
  Pallas kernels: 43.7 us -> 42.3 us
    pallas_call x1, Pallas kernels: 43.7 us -> 42.3 us  [per_device(): pl.pallas_call(functools.partial(kernel, dims), out_shape=jax.ShapeDtypeS...]
where the time goes in v2:
time: 44 us; the launch traced here: 43.9 us
  Pallas kernels  42.3 us (96%)
  local copies, waits for them, and re-layouts  1.59 us (4%)
    pallas_call x1, Pallas kernels, per_device(): pl.pallas_call(functools.partial(kernel, dims), out_shape=jax.ShapeDtypeS...  42.3 us
    unnamed x1, local copies, waits for them, and re-layouts  1.59 us

profile of v2, /device:TPU:0, one launch (start us, length us, event | category | flops | bytes accessed | tf_op | source)
XLA Modules:
  0.0 43.9 jit_solution(790944782207834176)
XLA Ops:
  0.0 42.3 %shard_map.55 = f32[4,6,4,384]{3,2,1,0:T(4,128)} custom-call(s32[3,16]{1,0:T(4,128)} %src_hbm.1, s32[3,16]{1,0:T(4,128)} %dst_hbm.1, f32[4,6,4,384]{3,2,1,0:T(4,128)} %rs_hbm.1, bf16[4,6,384,384]{3,2,1,0:T(8,128)(2,1)} %diag_hbm.1, bf16[3,16,384,384]{3,2,1,0:T(8,128)(2,1)} %panel_hbm.1), custom_call_target="tpu_custom_call" | custom-call | tf_op jit(solution)/shard_map/pallas_call | solution.py:437
  42.3 1.6 %copy.7 = f32[4,6,4,384]{3,2,1,0:T(4,128)} copy(f32[4,6,4,384]{3,2,1,0:T(4,128)} %shard_map.55) | data formatting | bytes 294912

commit v3 on v2

--- a/solution.py
+++ b/solution.py
@@ -42,8 +42,7 @@
     rows = SLOTS * block
     pairs = 2 * HOOD
     senders = HOOD * rep_size
-    half_rows = 2 * cols
-    third = width // 3
+    half_rows = cols
     own_rows = tiles * cols
     last = levels - 2
     zero_tile = (levels - 1) * tiles
@@ -54,6 +53,7 @@
     partner = me_r + 1 - 2 * my_half
     offsets = [o - HALF for o in range(HOOD - 1)] + [far]
     order = (HOOD - 1, 0, HOOD - 2, HALF, 1, HOOD - 3)
+    groups = ((1, 3), (0, 4), (5, 2))
 
     def peer_dom(offset):
         return lax.rem(me_d + (offset + dom_size), dom_size)
@@ -62,7 +62,7 @@
         return lax.rem(me_r + step, rep_size)
 
     peers = [(j, side) for j in order for side in (1, 0) if (offsets[j], side) != (0, 0)]
-    others = [s for s in range(2, rep_size)] + [1]
+    others = list(range(1, rep_size))
     everyone = [(j, step) for j in order for step in others + [0] if (offsets[j], step) != (0, 0)]
 
     def load_diag(level):
@@ -272,11 +272,9 @@
         span = senders * half_rows
         lane = iota((1, span), 1)
         lane_in = lane - half_rows * div(lane, half_rows)
-        low = lane_in < cols
         full = full.astype(BF16)
-        first = lookup(full, senders, span, lane_in + last * rows)
-        fold = lookup(full, senders, span, lane_in + last * rows + jnp.where(low, 2.0 * cols, 1.0 * cols))
-        for i, goal in enumerate((first, jnp.where(low, fold, -1.0), jnp.where(low, -1.0, fold))):
+        for i in range(SLOTS):
+            goal = lookup(full, senders, span, lane_in + (last * rows + i * cols))
             last_unpack[i] = jnp.where(iota((own_rows, span), 0) == goal, 1.0, 0.0).astype(BF16)
 
     def emit(level):
@@ -342,39 +340,39 @@
             slot_copy.wait()
         for part in range(panels // chunk):
             load_panel(level, part).wait()
-        for j in order:
-            products = []
-            for k in range(SLOTS):
-                which = jnp.clip(slots_s[2 * level, j * SLOTS + k], 0, panels - 1)
-                source = jnp.clip(slots_s[2 * level + 1, j * SLOTS + k], 0, zero_tile)
-                products.append(
-                    jnp.dot(
+        for group in groups:
+            products = {}
+            for j in group:
+                for k in range(SLOTS):
+                    which = jnp.clip(slots_s[2 * level, j * SLOTS + k], 0, panels - 1)
+                    source = jnp.clip(slots_s[2 * level + 1, j * SLOTS + k], 0, zero_tile)
+                    products[j, k] = jnp.dot(
                         store[source], panels_by_level[level][which], preferred_element_type=F32
                     )
-                )
+            for j in group:
+                if level < last:
+                    for k in range(SLOTS):
+                        rounded = products[j, k].astype(BF16)
+                        for h in range(2):
+                            val_send[level, h, j, k * block : (k + 1) * block] = rounded[
+                                h * block : (h + 1) * block
+                            ]
+                else:
+                    for r in range(rep_size):
+                        begin = r % 2 * block + r // 2 * cols
+                        piece = [products[j, k][begin : begin + cols] for k in range(SLOTS)]
+                        for k in range(SLOTS):
+                            last_send[j, r, :, k * width : (k + 1) * width] = piece[k].astype(BF16)
             if level < last:
-                for k in range(SLOTS):
-                    rounded = products[k].astype(BF16)
-                    for h in range(2):
-                        val_send[level, h, j, k * block : (k + 1) * block] = rounded[
-                            h * block : (h + 1) * block
-                        ]
                 for side in (1, 0):
-                    if (j, side) in peers:
-                        send_val(level, j, side).start()
+                    for j in group:
+                        if (j, side) in peers:
+                            send_val(level, j, side).start()
             else:
-                for r in range(rep_size):
-                    begin = r % 2 * block + r // 2 * cols
-                    piece = [p[begin : begin + cols] for p in products]
-                    last_send[j, r, :, :width] = jnp.concatenate(piece[:2], axis=0).astype(BF16)
-                    tail = piece[2]
-                    mixed = jnp.concatenate([tail[:, :third], tail[:, 2 * third :]], axis=0)
-                    again = jnp.concatenate([tail[:, third : 2 * third]] * 2, axis=0)
-                    last_send[j, r, :, width : width + third] = mixed.astype(BF16)
-                    last_send[j, r, :, width + third :] = again.astype(BF16)
                 for step in others + [0]:
-                    if (j, step) in everyone:
-                        send_last(j, step).start()
+                    for j in group:
+                        if (j, step) in everyone:
+                            send_last(j, step).start()
         if level < last:
             val_recv[level, HALF, my_half] = val_send[level, my_half, HALF]
         else:
@@ -395,12 +393,12 @@
 
     for j, step in everyone:
         await_last(j, step)
-    arrived = last_recv[...].reshape(senders * half_rows, width + 2 * third)
-    folded = arrived[:, width:]
-    whole = jnp.dot(last_unpack[0], arrived[:, :width], preferred_element_type=F32)
-    low = jnp.dot(last_unpack[1], folded, preferred_element_type=F32)
-    high = jnp.dot(last_unpack[2], folded[:, :third], preferred_element_type=F32)
-    residual = own_sides(levels - 1) - (whole + jnp.concatenate([low, high], axis=1))
+    arrived = last_recv[...].reshape(senders * half_rows, SLOTS * width)
+    residual = own_sides(levels - 1)
+    for i in range(SLOTS):
+        residual = residual - jnp.dot(
+            last_unpack[i], arrived[:, i * width : (i + 1) * width], preferred_element_type=F32
+        )
     residual = residual.astype(BF16)
     load_diag(levels - 1).wait()
     for t in range(tiles):
@@ -459,9 +457,9 @@
             pltpu.VMEM((levels - 1, rep_size, tile_rows, width), BF16),
             pltpu.VMEM((HOOD, 1, 128), i32),
             pltpu.VMEM((HOOD, rep_size, 1, 128), i32),
-            pltpu.VMEM((HOOD, rep_size, 2 * cols, width + width // 3 * 2), BF16),
-            pltpu.VMEM((HOOD, rep_size, 2 * cols, width + width // 3 * 2), BF16),
-            pltpu.VMEM((3, tiles * cols, HOOD * rep_size * 2 * cols), BF16),
+            pltpu.VMEM((HOOD, rep_size, cols, SLOTS * width), BF16),
+            pltpu.VMEM((HOOD, rep_size, cols, SLOTS * width), BF16),
+            pltpu.VMEM((SLOTS, tiles * cols, HOOD * rep_size * cols), BF16),
             dma((levels,)),
             dma((levels - 1, panels // chunk)),
             dma((levels - 2, HOOD, 2)),

time: 44 us -> 41.5 us (0.943)
  Pallas kernels: 42.3 us -> 39.8 us
    pallas_call x1, Pallas kernels: 42.3 us -> 39.8 us  [per_device(): pl.pallas_call(functools.partial(kernel, dims), out_shape=jax.ShapeDtypeS...]
where the time goes in v3:
time: 41.5 us; the launch traced here: 41.4 us
  Pallas kernels  39.8 us (96%)
  local copies, waits for them, and re-layouts  1.59 us (4%)
    pallas_call x1, Pallas kernels, per_device(): pl.pallas_call(functools.partial(kernel, dims), out_shape=jax.ShapeDtypeS...  39.8 us
    unnamed x1, local copies, waits for them, and re-layouts  1.59 us

profile of v3, /device:TPU:0, one launch (start us, length us, event | category | flops | bytes accessed | tf_op | source)
XLA Modules:
  0.0 41.4 jit_solution(7590926785489690785)
XLA Ops:
  0.0 39.8 %shard_map.55 = f32[4,6,4,384]{3,2,1,0:T(4,128)} custom-call(s32[3,16]{1,0:T(4,128)} %src_hbm.1, s32[3,16]{1,0:T(4,128)} %dst_hbm.1, f32[4,6,4,384]{3,2,1,0:T(4,128)} %rs_hbm.1, bf16[4,6,384,384]{3,2,1,0:T(8,128)(2,1)} %diag_hbm.1, bf16[3,16,384,384]{3,2,1,0:T(8,128)(2,1)} %panel_hbm.1), custom_call_target="tpu_custom_call" | custom-call | tf_op jit(solution)/shard_map/pallas_call | solution.py:435
  39.8 1.6 %copy.7 = f32[4,6,4,384]{3,2,1,0:T(4,128)} copy(f32[4,6,4,384]{3,2,1,0:T(4,128)} %shard_map.55) | data formatting | bytes 294912

commit v4 on v3

--- a/solution.py
+++ b/solution.py
@@ -31,9 +31,9 @@
     diag, panels_by_level, store, solved_ref, placed,
     slots_v, slots_s, slot_sem,
     val_send, val_recv, unpack, part_send, part_recv, id_send, id_recv,
-    last_send, last_recv, last_unpack,
+    unit_send, unit_recv, unit_unpack, last_send, last_recv,
     diag_sem, panel_sem, val_ssem, val_rsem, part_ssem, part_rsem, id_ssem, id_rsem,
-    last_ssem, last_rsem,
+    unit_ssem, unit_rsem, last_ssem, last_rsem,
 ):
     levels, tiles, cols, width, panels, dom_size, rep_size, chunk = dims
     far = dom_size // 2
@@ -48,12 +48,19 @@
     zero_tile = (levels - 1) * tiles
     me_d = lax.axis_index("dom")
     me_r = lax.axis_index("rep")
-    my_half = lax.rem(me_r, 2)
-    my_place = me_r // 2
-    partner = me_r + 1 - 2 * my_half
+    ends, inner = (0, rep_size - 1), (1, rep_size - 2)
+    ranking = ends + inner
+    my_side = me_r // 2
+    my_end = my_side * (rep_size - 1)
+    my_turn = lax.rem(me_r, 2)
+    my_unit = lax.rem(me_r + 1, 2)
+    my_half = lax.rem((me_r + 1) // 2, 2)
+    is_end = my_half == 0
+    is_inner = my_half == 1
     offsets = [o - HALF for o in range(HOOD - 1)] + [far]
     order = (HOOD - 1, 0, HOOD - 2, HALF, 1, HOOD - 3)
-    groups = ((1, 3), (0, 4), (5, 2))
+    val_groups = ((1, 3), (0, 4), (2, 5))
+    last_groups = ((0, 4), (1, 3), (5, 2))
 
     def peer_dom(offset):
         return lax.rem(me_d + (offset + dom_size), dom_size)
@@ -61,7 +68,6 @@
     def peer_rep(step):
         return lax.rem(me_r + step, rep_size)
 
-    peers = [(j, side) for j in order for side in (1, 0) if (offsets[j], side) != (0, 0)]
     others = list(range(1, rep_size))
     everyone = [(j, step) for j in order for step in others + [0] if (offsets[j], step) != (0, 0)]
 
@@ -74,11 +80,12 @@
             panel_hbm.at[level, span], panels_by_level[level].at[span], panel_sem.at[level, part]
         )
 
-    def side_rep(side):
-        return partner if side else me_r
-
-    def side_half(side):
-        return 1 - my_half if side else my_half
+    def aim(step):
+        if step == 0:
+            return me_r
+        end_aim = jnp.where(me_r == 0, rep_size - step, step - 1)
+        inner_aim = ((rep_size - 1 - my_end, rep_size - 1 - me_r, my_end)[step - 1])
+        return jnp.where(is_end, end_aim, inner_aim)
 
     def send_id(j, step):
         return pltpu.make_async_remote_copy(
@@ -122,49 +129,83 @@
             device_id_type=MESH,
         ).wait_recv()
 
-    def send_val(level, j, side):
+    def send_val(level, j):
         return pltpu.make_async_remote_copy(
-            src_ref=val_send.at[level, side_half(side), j],
-            dst_ref=val_recv.at[level, j, my_half],
-            send_sem=val_ssem.at[level, j, side],
-            recv_sem=val_rsem.at[level, j, my_half],
-            device_id=(peer_dom(offsets[j]), side_rep(side)),
-            device_id_type=MESH,
-        )
-
-    def await_val(level, j, side):
+            src_ref=val_send.at[level, j],
+            dst_ref=val_recv.at[level, j, my_turn],
+            send_sem=val_ssem.at[level, j],
+            recv_sem=val_rsem.at[level, j, my_turn],
+            device_id=(peer_dom(offsets[j]), my_end),
+            device_id_type=MESH,
+        )
+
+    def await_val(level, j, other):
+        turn = 1 - my_turn if other else my_turn
         pltpu.make_async_remote_copy(
-            src_ref=val_send.at[level, side_half(side), j],
-            dst_ref=val_recv.at[level, j, side_half(side)],
-            send_sem=val_ssem.at[level, j, side],
-            recv_sem=val_rsem.at[level, j, side_half(side)],
-            device_id=(peer_dom(-offsets[j]), side_rep(side)),
+            src_ref=val_send.at[level, j],
+            dst_ref=val_recv.at[level, j, turn],
+            send_sem=val_ssem.at[level, j],
+            recv_sem=val_rsem.at[level, j, turn],
+            device_id=(peer_dom(-offsets[j]), 2 * my_side + turn),
             device_id_type=MESH,
         ).wait_recv()
 
-    def part_span(level):
-        return pl.ds(0, tile_rows if level else own_rows)
-
-    def send_part(level, step):
+    def send_unit(level, j, m):
         return pltpu.make_async_remote_copy(
-            src_ref=part_send.at[level, part_span(level)],
-            dst_ref=part_recv.at[level, me_r, part_span(level)],
+            src_ref=unit_send.at[level, j, m],
+            dst_ref=unit_recv.at[level, j, me_r],
+            send_sem=unit_ssem.at[level, j, m],
+            recv_sem=unit_rsem.at[level, j, me_r],
+            device_id=(peer_dom(offsets[j]), jnp.int32(inner[m])),
+            device_id_type=MESH,
+        )
+
+    def await_unit(level, j, step):
+        slot = peer_rep(step)
+        pltpu.make_async_remote_copy(
+            src_ref=unit_send.at[level, j, 0],
+            dst_ref=unit_recv.at[level, j, slot],
+            send_sem=unit_ssem.at[level, j, 0],
+            recv_sem=unit_rsem.at[level, j, slot],
+            device_id=(peer_dom(-offsets[j]), slot),
+            device_id_type=MESH,
+        ).wait_recv()
+
+    def each_val(level, group, act):
+        for j in group:
+            for m in range(2):
+                if offsets[j] != 0:
+                    act(send_unit(level, j, m))
+                else:
+                    pl.when(me_r != inner[m])(lambda: act(send_unit(level, j, m)))
+        for j in group:
+            if offsets[j] != 0:
+                act(send_val(level, j))
+            else:
+                pl.when(is_inner)(lambda: act(send_val(level, j)))
+
+    def send_part(level, step, count):
+        return pltpu.make_async_remote_copy(
+            src_ref=part_send.at[level, pl.ds(0, count)],
+            dst_ref=part_recv.at[level, me_r, pl.ds(0, count)],
             send_sem=part_ssem.at[level, step],
             recv_sem=part_rsem.at[level, me_r],
-            device_id=(me_d, peer_rep(step)),
-            device_id_type=MESH,
-        )
-
-    def await_part(level, step):
-        slot = peer_rep(step)
+            device_id=(me_d, aim(step)),
+            device_id_type=MESH,
+        )
+
+    def await_part(level, rep, count):
         pltpu.make_async_remote_copy(
-            src_ref=part_send.at[level, part_span(level)],
-            dst_ref=part_recv.at[level, slot, part_span(level)],
-            send_sem=part_ssem.at[level, step],
-            recv_sem=part_rsem.at[level, slot],
-            device_id=(me_d, slot),
+            src_ref=part_send.at[level, pl.ds(0, count)],
+            dst_ref=part_recv.at[level, rep, pl.ds(0, count)],
+            send_sem=part_ssem.at[level, 1],
+            recv_sem=part_rsem.at[level, rep],
+            device_id=(me_d, jnp.int32(rep)),
             device_id_type=MESH,
         ).wait_recv()
+
+    def count_of(level, rep):
+        return tile_rows if level and rep in ends else own_rows
 
     small = [
         pltpu.make_async_copy(hbm, ref, small_sem.at[i])
@@ -189,24 +230,23 @@
         row = lax.broadcasted_iota(jnp.int32, (block, width), 0) // cols
         for t in range(tiles):
             twice = jnp.concatenate([rs_ref[level, t]] * (rep_size // 2), axis=0)
-            placed[level, t * block : (t + 1) * block] = jnp.where(row == my_place, twice, 0.0)
+            placed[level, t * block : (t + 1) * block] = jnp.where(row == my_side, twice, 0.0)
 
     def share(level, partial):
         rounded = partial.astype(BF16)
-        part_send[level, : rounded.shape[0]] = rounded
+        count = rounded.shape[0]
+        part_send[level, :count] = rounded
         for step in others:
-            send_part(level, step).start()
-        part_recv[level, me_r, : rounded.shape[0]] = rounded
+            send_part(level, step, count).start()
+        part_recv[level, me_r, :count] = rounded
 
     def route():
         owner = me_d.astype(F32)
         row16 = iota((panels, panels), 0)
         col16 = iota((panels, panels), 1)
         lane = iota((1, 128), 1)
-        id_level = div(lane, rows)
-        id_rest = lane - rows * id_level
-        id_slot = div(id_rest, block)
-        id_col = id_rest - block * id_slot
+        id_level = div(lane, SLOTS)
+        id_slot = lane - SLOTS * id_level
         panel_col = iota((panels, 1), 0)
         wanted = [jnp.zeros((1, 128), F32) for _ in range(HOOD)]
         for l in range(levels - 1):
@@ -231,13 +271,9 @@
             source = jnp.sum(jnp.where(here, scol - zero_tile, 0.0), axis=0, keepdims=True)
             slots_v[2 * l : 2 * l + 1, :] = which.astype(jnp.int32)
             slots_v[2 * l + 1 : 2 * l + 2, :] = (source + zero_tile).astype(jnp.int32)
-            if l == last:
-                id_slot = div(id_rest, cols)
-                id_col = id_rest - cols * id_slot
             mine = (rank == id_slot) & (id_level == l)
             for j in range(HOOD):
-                spread = tile * (cols if l == last else block) + id_col + 1.0
-                found = jnp.where(mine & (reach == j), spread, 0.0)
+                found = jnp.where(mine & (reach == j), tile + 1.0, 0.0)
                 wanted[j] = wanted[j] + jnp.sum(found, axis=0, keepdims=True)
         for j in range(HOOD):
             id_send[j] = (wanted[j] - 1.0).astype(jnp.int32)
@@ -257,32 +293,48 @@
         near = jnp.zeros((pairs, 128), F32)
         full = jnp.zeros((senders, 128), F32)
         for j in range(HOOD):
-            for side in range(2):
-                row = id_recv[j, my_place * 2 + side].astype(F32)
-                near = jnp.where(iota((pairs, 128), 0) == 2 * j + side, row, near)
+            for turn in range(2):
+                row = id_recv[j, 2 * my_side + turn].astype(F32)
+                near = jnp.where(iota((pairs, 128), 0) == 2 * j + turn, row, near)
             for r in range(rep_size):
                 row = id_recv[j, r].astype(F32)
                 full = jnp.where(iota((senders, 128), 0) == rep_size * j + r, row, full)
+        near, full = near.astype(BF16), full.astype(BF16)
         span = pairs * rows
         lane = iota((1, span), 1)
         lane_in = lane - rows * div(lane, rows)
+        lane_slot = div(lane_in, block)
+        lane_col = lane_in - block * lane_slot
         for l in range(last):
-            goal = lookup(near.astype(BF16), pairs, span, lane_in + l * rows)
+            tile = lookup(near, pairs, span, lane_slot + l * SLOTS)
+            goal = jnp.where(tile >= 0, tile * block + lane_col, -1.0)
             unpack[l] = jnp.where(iota((tile_rows, span), 0) == goal, 1.0, 0.0).astype(BF16)
-        span = senders * half_rows
+        span = senders * cols
         lane = iota((1, span), 1)
-        lane_in = lane - half_rows * div(lane, half_rows)
-        full = full.astype(BF16)
-        for i in range(SLOTS):
-            goal = lookup(full, senders, span, lane_in + (last * rows + i * cols))
-            last_unpack[i] = jnp.where(iota((own_rows, span), 0) == goal, 1.0, 0.0).astype(BF16)
+        lane_col = lane - cols * div(lane, cols)
+        for l in range(levels - 1):
+            for k in range(SLOTS):
+                tile = lookup(full, senders, span, jnp.full((1, span), float(l * SLOTS + k), F32))
+                goal = jnp.where(tile >= 0, tile * cols + lane_col, -1.0)
+                unit_unpack[l, k] = jnp.where(iota((own_rows, span), 0) == goal, 1.0, 0.0).astype(BF16)
+
+    def gather_units(level, arrived):
+        residual = own_sides(level + 1)
+        arrived = arrived.reshape(senders * cols, SLOTS * width)
+        for k in range(SLOTS):
+            residual = residual - jnp.dot(
+                unit_unpack[level, k],
+                arrived[:, k * width : (k + 1) * width],
+                preferred_element_type=F32,
+            )
+        return residual
 
     def emit(level):
         for t in range(tiles):
             mine = solved_ref[level, t, my_half]
             picked = mine[:cols]
             for q in range(1, rep_size // 2):
-                picked = jnp.where(my_place == q, mine[q * cols : (q + 1) * cols], picked)
+                picked = jnp.where(my_side == q, mine[q * cols : (q + 1) * cols], picked)
             out_ref[level, t] = picked
 
     def own_sides(level):
@@ -303,30 +355,25 @@
     store[zero_tile] = jnp.zeros((2 * block, width), BF16)
 
     for level in range(levels - 1):
-        for step in others:
-            await_part(level, step)
+        for r in range(rep_size):
+            pl.when(me_r != r)(lambda: await_part(level, r, count_of(level, r)))
         if level == 0:
             parts = [part_recv[0, r, :own_rows].astype(F32) for r in range(rep_size)]
             residuals = [
                 jnp.concatenate(
-                    [
-                        parts[r][t * cols : (t + 1) * cols]
-                        for h in range(2)
-                        for r in range(h, rep_size, 2)
-                    ],
-                    axis=0,
+                    [parts[r][t * cols : (t + 1) * cols] for r in ranking], axis=0
                 )
                 for t in range(tiles)
             ]
         else:
-            halves = []
-            for h in range(2):
-                total = part_recv[level, h].astype(F32)
-                for r in range(h + 2, rep_size, 2):
-                    total = total + part_recv[level, r].astype(F32)
-                halves.append(total)
+            total = part_recv[level, ends[0]].astype(F32) + part_recv[level, ends[1]].astype(F32)
+            parts = [part_recv[level, r, :own_rows].astype(F32) for r in inner]
             residuals = [
-                jnp.concatenate([half[t * block : (t + 1) * block] for half in halves], axis=0)
+                jnp.concatenate(
+                    [total[t * block : (t + 1) * block]]
+                    + [part[t * cols : (t + 1) * cols] for part in parts],
+                    axis=0,
+                )
                 for t in range(tiles)
             ]
         load_diag(level).wait()
@@ -340,7 +387,7 @@
             slot_copy.wait()
         for part in range(panels // chunk):
             load_panel(level, part).wait()
-        for group in groups:
+        for group in val_groups if level < last else last_groups:
             products = {}
             for j in group:
                 for k in range(SLOTS):
@@ -353,28 +400,35 @@
                 if level < last:
                     for k in range(SLOTS):
                         rounded = products[j, k].astype(BF16)
-                        for h in range(2):
-                            val_send[level, h, j, k * block : (k + 1) * block] = rounded[
-                                h * block : (h + 1) * block
-                            ]
+                        val_send[level, j, k * block : (k + 1) * block] = rounded[:block]
+                        for m in range(2):
+                            begin = block + m * cols
+                            unit_send[level, j, m, :, k * width : (k + 1) * width] = products[j, k][
+                                begin : begin + cols
+                            ].astype(BF16)
                 else:
                     for r in range(rep_size):
-                        begin = r % 2 * block + r // 2 * cols
+                        begin = ranking.index(r) * cols
                         piece = [products[j, k][begin : begin + cols] for k in range(SLOTS)]
                         for k in range(SLOTS):
                             last_send[j, r, :, k * width : (k + 1) * width] = piece[k].astype(BF16)
             if level < last:
-                for side in (1, 0):
-                    for j in group:
-                        if (j, side) in peers:
-                            send_val(level, j, side).start()
+                each_val(level, group, lambda copy: copy.start())
             else:
                 for step in others + [0]:
                     for j in group:
                         if (j, step) in everyone:
                             send_last(j, step).start()
         if level < last:
-            val_recv[level, HALF, my_half] = val_send[level, my_half, HALF]
+
+            @pl.when(is_end)
+            def _():
+                val_recv[level, HALF, my_turn] = val_send[level, HALF]
+
+            @pl.when(is_inner)
+            def _():
+                unit_recv[level, HALF, me_r] = unit_send[level, HALF, my_unit]
+
         else:
             last_recv[HALF, me_r] = last_send[HALF, me_r]
         load_diag(level + 1).start()
@@ -385,20 +439,26 @@
             learn_ids()
         emit(level)
         if level < last:
-            for j, side in peers:
-                await_val(level, j, side)
-            arrived = val_recv[level].reshape(pairs * rows, width)
-            incoming = jnp.dot(unpack[level], arrived, preferred_element_type=F32)
-            share(level + 1, placed[level + 1] - incoming)
+
+            @pl.when(is_end)
+            def _():
+                for j in order:
+                    for other in (True, False):
+                        if other or offsets[j] != 0:
+                            await_val(level, j, other)
+                arrived = val_recv[level].reshape(pairs * rows, width)
+                incoming = jnp.dot(unpack[level], arrived, preferred_element_type=F32)
+                share(level + 1, placed[level + 1] - incoming)
+
+            @pl.when(is_inner)
+            def _():
+                for j, step in everyone:
+                    await_unit(level, j, step)
+                share(level + 1, gather_units(level, unit_recv[level]))
 
     for j, step in everyone:
         await_last(j, step)
-    arrived = last_recv[...].reshape(senders * half_rows, SLOTS * width)
-    residual = own_sides(levels - 1)
-    for i in range(SLOTS):
-        residual = residual - jnp.dot(
-            last_unpack[i], arrived[:, i * width : (i + 1) * width], preferred_element_type=F32
-        )
+    residual = gather_units(last, last_recv[...])
     residual = residual.astype(BF16)
     load_diag(levels - 1).wait()
     for t in range(tiles):
@@ -408,12 +468,13 @@
     for j, step in everyone:
         send_id(j, step).wait_send()
         send_last(j, step).wait_send()
-    for j, side in peers:
-        for level in range(last):
-            send_val(level, j, side).wait_send()
+    for level in range(last):
+        each_val(level, order, lambda copy: copy.wait_send())
     for step in others:
-        for level in range(levels - 1):
-            send_part(level, step).wait_send()
+        send_part(0, step, own_rows).wait_send()
+        for level in range(1, levels - 1):
+            pl.when(is_end)(lambda: send_part(level, step, tile_rows).wait_send())
+            pl.when(is_inner)(lambda: send_part(level, step, own_rows).wait_send())
 
 
 def per_device(right_sides, diag_inverse, panel_mats, panel_src, panel_dst):
@@ -425,8 +486,7 @@
     tile_rows = tiles * block
     rows = SLOTS * block
     chunk = 4 if panels % 4 == 0 else 1
-    assert rep_size % 2 == 0 and block % 8 == 0 and (levels - 1) * rows <= 128
-    assert 2 * cols == 8 and width % 384 == 0 and levels > 2
+    assert rep_size == 4 and block % 8 == 0 and (levels - 1) * SLOTS <= 128 and levels > 2
     dims = (levels, tiles, cols, width, panels, dom_size, rep_size, chunk)
     vmem = pl.BlockSpec(memory_space=pltpu.VMEM)
     hbm = pl.BlockSpec(memory_space=pl.ANY)
@@ -450,24 +510,28 @@
             pltpu.VMEM((8, 128), i32),
             pltpu.SMEM((8, 128), i32),
             dma,
-            pltpu.VMEM((levels - 2, 2, HOOD, rows, width), BF16),
+            pltpu.VMEM((levels - 2, HOOD, rows, width), BF16),
             pltpu.VMEM((levels - 2, HOOD, 2, rows, width), BF16),
             pltpu.VMEM((levels - 2, tile_rows, 2 * HOOD * rows), BF16),
             pltpu.VMEM((levels - 1, tile_rows, width), BF16),
             pltpu.VMEM((levels - 1, rep_size, tile_rows, width), BF16),
             pltpu.VMEM((HOOD, 1, 128), i32),
             pltpu.VMEM((HOOD, rep_size, 1, 128), i32),
+            pltpu.VMEM((levels - 2, HOOD, 2, cols, SLOTS * width), BF16),
+            pltpu.VMEM((levels - 2, HOOD, rep_size, cols, SLOTS * width), BF16),
+            pltpu.VMEM((levels - 1, SLOTS, tiles * cols, HOOD * rep_size * cols), BF16),
             pltpu.VMEM((HOOD, rep_size, cols, SLOTS * width), BF16),
             pltpu.VMEM((HOOD, rep_size, cols, SLOTS * width), BF16),
-            pltpu.VMEM((SLOTS, tiles * cols, HOOD * rep_size * cols), BF16),
             dma((levels,)),
             dma((levels - 1, panels // chunk)),
-            dma((levels - 2, HOOD, 2)),
+            dma((levels - 2, HOOD)),
             dma((levels - 2, HOOD, 2)),
             dma((levels - 1, rep_size)),
             dma((levels - 1, rep_size)),
             dma((HOOD, rep_size)),
             dma((HOOD, rep_size)),
+            dma((levels - 2, HOOD, 2)),
+            dma((levels - 2, HOOD, rep_size)),
             dma((HOOD, rep_size)),
             dma((HOOD, rep_size)),
         ],

time: 41.5 us -> 40.5 us (0.976)
  Pallas kernels: 39.8 us -> 38.8 us
    pallas_call x1, Pallas kernels: 39.8 us -> 38.8 us  [per_device(): pl.pallas_call(functools.partial(kernel, dims), out_shape=jax.ShapeDtypeS...]
where the time goes in v4:
time: 40.5 us; the launch traced here: 40.3 us
  Pallas kernels  38.8 us (96%)
  local copies, waits for them, and re-layouts  1.59 us (4%)
    pallas_call x1, Pallas kernels, per_device(): pl.pallas_call(functools.partial(kernel, dims), out_shape=jax.ShapeDtypeS...  38.8 us
    unnamed x1, local copies, waits for them, and re-layouts  1.59 us

profile of v4, /device:TPU:0, one launch (start us, length us, event | category | flops | bytes accessed | tf_op | source)
XLA Modules:
  0.0 40.3 jit_solution(3444747061387970073)
XLA Ops:
  0.0 38.8 %shard_map.55 = f32[4,6,4,384]{3,2,1,0:T(4,128)} custom-call(s32[3,16]{1,0:T(4,128)} %src_hbm.1, s32[3,16]{1,0:T(4,128)} %dst_hbm.1, f32[4,6,4,384]{3,2,1,0:T(4,128)} %rs_hbm.1, bf16[4,6,384,384]{3,2,1,0:T(8,128)(2,1)} %diag_hbm.1, bf16[3,16,384,384]{3,2,1,0:T(8,128)(2,1)} %panel_hbm.1), custom_call_target="tpu_custom_call" | custom-call | tf_op jit(solution)/shard_map/pallas_call | solution.py:495
  38.8 1.6 %copy.7 = f32[4,6,4,384]{3,2,1,0:T(4,128)} copy(f32[4,6,4,384]{3,2,1,0:T(4,128)} %shard_map.55) | data formatting | bytes 294912

commit v5 on v4

--- a/solution.py
+++ b/solution.py
@@ -151,12 +151,13 @@
         ).wait_recv()
 
     def send_unit(level, j, m):
+        target = 1 - my_side if m else my_side
         return pltpu.make_async_remote_copy(
-            src_ref=unit_send.at[level, j, m],
+            src_ref=unit_send.at[level, j, target],
             dst_ref=unit_recv.at[level, j, me_r],
             send_sem=unit_ssem.at[level, j, m],
             recv_sem=unit_rsem.at[level, j, me_r],
-            device_id=(peer_dom(offsets[j]), jnp.int32(inner[m])),
+            device_id=(peer_dom(offsets[j]), 1 + target),
             device_id_type=MESH,
         )
 
@@ -173,11 +174,12 @@
 
     def each_val(level, group, act):
         for j in group:
-            for m in range(2):
-                if offsets[j] != 0:
-                    act(send_unit(level, j, m))
-                else:
-                    pl.when(me_r != inner[m])(lambda: act(send_unit(level, j, m)))
+            act(send_unit(level, j, 1))
+        for j in group:
+            if offsets[j] != 0:
+                act(send_unit(level, j, 0))
+            else:
+                pl.when(is_end)(lambda: act(send_unit(level, j, 0)))
         for j in group:
             if offsets[j] != 0:
                 act(send_val(level, j))

time: 40.5 us -> 40.3 us (level)
  no operation moved by 1% of the time
where the time goes in v5:
time: 40.3 us; the launch traced here: 40.2 us
  Pallas kernels  38.6 us (96%)
  local copies, waits for them, and re-layouts  1.59 us (4%)
    pallas_call x1, Pallas kernels, per_device(): pl.pallas_call(functools.partial(kernel, dims), out_shape=jax.ShapeDtypeS...  38.6 us
    unnamed x1, local copies, waits for them, and re-layouts  1.59 us

profile of v5, /device:TPU:0, one launch (start us, length us, event | category | flops | bytes accessed | tf_op | source)
XLA Modules:
  0.0 40.2 jit_solution(14669389044147794085)
XLA Ops:
  0.0 38.6 %shard_map.55 = f32[4,6,4,384]{3,2,1,0:T(4,128)} custom-call(s32[3,16]{1,0:T(4,128)} %src_hbm.1, s32[3,16]{1,0:T(4,128)} %dst_hbm.1, f32[4,6,4,384]{3,2,1,0:T(4,128)} %rs_hbm.1, bf16[4,6,384,384]{3,2,1,0:T(8,128)(2,1)} %diag_hbm.1, bf16[3,16,384,384]{3,2,1,0:T(8,128)(2,1)} %panel_hbm.1), custom_call_target="tpu_custom_call" | custom-call | tf_op jit(solution)/shard_map/pallas_call | solution.py:497
  38.6 1.6 %copy.7 = f32[4,6,4,384]{3,2,1,0:T(4,128)} copy(f32[4,6,4,384]{3,2,1,0:T(4,128)} %shard_map.55) | data formatting | bytes 294912
